TPU v7x, 32 devices: a whole 2x2x4 slice. The times are simulated.
32 devices in a mesh: row: 4 (over y, core), col: 4 (over z), layer: 2 (over x).
Axes of the slice: x: 2, y: 2, z: 4, core: 2. Of those that a mesh axis runs over, the one named last changes fastest.
Arguments:
- a_tiles: float32 [16, 2, 7, 128, 128], P(('row', 'col'), 'layer'), may hold values from -0.5 to 0.5
- a_cols: int32 [16, 2, 7], P(('row', 'col'), 'layer'), may hold values from -1 to 255, as said below
- b_tiles: float32 [256, 2, 7, 128, 128], P(('row', 'col'), 'layer'), may hold values from -6 to 6
- b_rows: int32 [256, 2, 7], P(('row', 'col'), 'layer'), may hold values from 0 to 255, as said below
- c_cols: int32 [16, 4, 4], P('row', 'col'), may hold values from 0 to 255, as said below
Outputs:
- c_tiles: float32 [16, 4, 4, 128, 128], P('row', 'col', 'layer')
Inputs may be any that keep to these rules, and one draw needn't show every extreme that they name: In a_cols[i, h, :] the used slots come first and hold distinct block columns in [h * 128, (h + 1) * 128); the unused ones hold -1. Some block rows use all 7 slots in each half, others few. b_rows[j, h, :] holds 7 distinct block rows in [h * 128, (h + 1) * 128). c_cols[i, g, :] holds 4 distinct block columns j with (j // 16) % 4 == g.
All inputs are finite; a program needn't handle non-finite values.
Results may differ from a plain program's by a relative error of at most 0.0003.
Values sent between devices are 32-bit elements; how exact they have to be, the bound alone decides.
No kernel may reach another device: no remote copies, remote signals or barrier semaphores. Data moves between devices by JAX's collectives and lax.ppermute only.
A program may use at most 128 MiB of HBM per device.

v0:
```python
import jax
import jax.numpy as jnp
from jax import lax
from jax.sharding import PartitionSpec as P


def row_block(a_row, a_index, wanted, b_flat, b_index, block_width, group_count):
    halves = b_index.shape[1]
    slot_count = b_index.shape[2]
    panel_col = wanted // block_width // group_count * block_width + wanted % block_width
    col_rows = b_index[panel_col]
    matches = (col_rows[:, :, None, :] == a_index[None, :, :, None]) & (a_index >= 0)[
        None, :, :, None
    ]
    present = jnp.any(matches, axis=3)
    position = jnp.argmax(matches, axis=3)
    layer_ids = jnp.arange(halves, dtype=jnp.int32)
    flat_index = (
        panel_col[:, None, None] * halves + layer_ids[None, :, None]
    ) * slot_count + position
    chosen = jnp.take(b_flat, flat_index.reshape(-1), axis=0)
    chosen = chosen.reshape(flat_index.shape + b_flat.shape[1:])
    chosen = jnp.where(present[..., None, None], chosen, jnp.zeros((), chosen.dtype))
    return jnp.einsum("heab,qhebc->qac", a_row, chosen, precision=lax.Precision.HIGHEST)


def on_device(a_tiles, a_cols, b_tiles, b_rows, c_cols):
    block_width = b_tiles.shape[0]
    group_count = lax.axis_size("col")
    wanted = c_cols[:, 0, :]
    b_panel, b_index = (
        lax.all_gather(b_tiles, "row", axis=0, tiled=True),
        lax.all_gather(b_rows, "row", axis=0, tiled=True),
    )
    b_flat = b_panel.reshape((-1,) + b_panel.shape[3:])
    a_piece = lax.all_gather(a_tiles, "col", axis=0, tiled=True)
    index_piece = lax.all_gather(a_cols, "col", axis=0, tiled=True)

    def one_row(inputs):
        return row_block(inputs[0], inputs[1], inputs[2], b_flat, b_index, block_width, group_count)

    row_out = lax.map(one_row, (a_piece, index_piece, wanted))
    return lax.psum_scatter(row_out[:, None], "layer", scatter_dimension=2, tiled=True)


def solution(mesh):
    return jax.shard_map(
        on_device,
        mesh=mesh,
        in_specs=(
            P(("row", "col"), "layer", None, None, None),
            P(("row", "col"), "layer", None),
            P(("row", "col"), "layer", None, None, None),
            P(("row", "col"), "layer", None),
            P("row", "col", None),
        ),
        out_specs=P("row", "col", "layer", None, None),
        check_vma=False,
    )
```

profile of v0, /device:TPU:0, one launch (start us, length us, event | category | flops | bytes accessed | tf_op | source)
XLA Modules:
  0.0 355.9 jit_solution(14244354219094431181)
XLA Ops:
  8.1 12.6 %all_gather.13 = s32[4,1,7]{2,1,0:T(1,128)S(1)} all-gather(s32[1,1,7]{2,1,0:T(1,128)S(1)} %copy-done.1), channel_id=1, replica_groups=mesh['row'=4,'col'=4,'layer'=2] {'col'}, dimensions={0}, use_global_device_ids=true | all-gather | bytes 140 | tf_op jit(solution)/shard_map/all_gather | solution.py:37
  20.8 5.2 %all_gather.12 = s32[64,1,7]{2,0,1:T(8,128)S(1)} all-gather(s32[16,1,7]{2,0,1:T(8,128)S(1)} %copy.18), channel_id=1, replica_groups=mesh['row'=4,'col'=4,'layer'=2] {'row'}, dimensions={0}, use_global_device_ids=true | all-gather | bytes 2240 | tf_op jit(solution)/shard_map/all_gather | solution.py:33
  26.0 27.0 %all-gather.5.cloned.1.call-done = f32[4,1,7,128,128]{4,3,2,1,0:T(8,128)} async-done(((f32[1,1,7,128,128]{4,3,2,1,0:T(8,128)}), f32[4,1,7,128,128]{4,3,2,1,0:T(8,128)}) %all-gather.5.cloned.1.call-update) | async-done | bytes 1835024 | tf_op jit(solution)/shard_map/all_gather | solution.py:36
  53.0 178.4 %all-gather.3.cloned.1.call-done = f32[64,1,7,128,128]{4,3,2,1,0:T(8,128)} async-done(((f32[16,1,7,128,128]{4,3,2,1,0:T(8,128)}), f32[64,1,7,128,128]{4,3,2,1,0:T(8,128)}) %all-gather.3.cloned.1.call-update) | async-done | bytes 29360144 | tf_op jit(solution)/shard_map/all_gather | solution.py:32
  231.4 75.8 %while.13 = (s32[]{:T(128)}, f32[4,4,128,128]{3,2,1,0:T(8,128)}, s32[4,4]{1,0:T(4,128)S(1)}, s32[64,1,7]{2,0,1:T(8,128)S(1)}, s32[4,1,7]{2,1,0:T(1,128)S(1)}, /*...) while((s32[]{:T(128)}, f32[4,4,128,128]{3,2,1,0:T(8,128)}, s32[4,4]{1,0:T(4,128)S(1)}, ...), condition=%wide.region_3.4_spmd, body=%wide.region_0.3_spmd.sunk | while | flops 705565312 | bytes 10955050 | solution.py:42
  232.4 1.0 iota_reduce_fusion.2
  233.6 11.3 %gather_fusion.1 = f32[28,128,128]{2,1,0:T(8,128)} fusion(f32[448,128,128]{2,1,0:T(8,128)} %get-tuple-element.214, s32[1024]{0:T(1024)S(1)} %pad_clamp_fusion.5), kind=kCustom, calls=%fused_computation.1.clone.1 | custom fusion | bytes 3670128 | tf_op jit(solution)/shard_map/while/body/eval_jaxpr/jit(_take)/gather | solution.py:21
  244.9 1.8 copy.30
  246.7 2.8 fusion.36
  249.6 0.7 constant_dynamic-update-slice_fusion.2
  251.4 1.0 iota_reduce_fusion.2
  252.6 11.3 %gather_fusion.1 = f32[28,128,128]{2,1,0:T(8,128)} fusion(f32[448,128,128]{2,1,0:T(8,128)} %get-tuple-element.214, s32[1024]{0:T(1024)S(1)} %pad_clamp_fusion.5), kind=kCustom, calls=%fused_computation.1.clone.1 | custom fusion | bytes 3670128 | tf_op jit(solution)/shard_map/while/body/eval_jaxpr/jit(_take)/gather | solution.py:21
  263.8 1.8 copy.30
  265.7 2.8 fusion.36
  270.3 1.0 iota_reduce_fusion.2
  271.5 11.3 %gather_fusion.1 = f32[28,128,128]{2,1,0:T(8,128)} fusion(f32[448,128,128]{2,1,0:T(8,128)} %get-tuple-element.214, s32[1024]{0:T(1024)S(1)} %pad_clamp_fusion.5), kind=kCustom, calls=%fused_computation.1.clone.1 | custom fusion | bytes 3670128 | tf_op jit(solution)/shard_map/while/body/eval_jaxpr/jit(_take)/gather | solution.py:21
  282.8 1.8 copy.30
  284.6 2.8 fusion.36
  289.3 1.0 iota_reduce_fusion.2
  290.5 11.3 %gather_fusion.1 = f32[28,128,128]{2,1,0:T(8,128)} fusion(f32[448,128,128]{2,1,0:T(8,128)} %get-tuple-element.214, s32[1024]{0:T(1024)S(1)} %pad_clamp_fusion.5), kind=kCustom, calls=%fused_computation.1.clone.1 | custom fusion | bytes 3670128 | tf_op jit(solution)/shard_map/while/body/eval_jaxpr/jit(_take)/gather | solution.py:21
  301.7 1.8 copy.30
  303.6 2.8 fusion.36
  308.5 39.0 %all-reduce.3.cloned.1.call-done = f32[4,1,4,128,128]{4,3,2,1,0:T(8,128)} async-done(((f32[4,1,4,128,128]{4,3,2,1,0:T(8,128)}), f32[4,1,4,128,128]{4,3,2,1,0:T(8,128)}) %all-reduce.3.cloned.1.call-update) | async-done | bytes 1048592
  347.5 1.9 constant_dynamic-slice_fusion.2
  (76 shorter events, 9.8 us)
Async XLA Ops:
  6.5 46.5 %all-gather.5.cloned.1.call-start = ((), (), s32[]{:S(2)}) async-start(), calls=%async_computation.1 | async-start | bytes 2293760 | tf_op jit(solution)/shard_map/all_gather | solution.py:36
  7.3 0.8 copy-start.1
  7.3 13.5 %copy-start = (s32[16,1,7]{0,1,2:T(1,128)S(1)}, s32[16,1,7]{0,1,2:T(1,128)}, u32[]{:S(2)}) copy-start(s32[16,1,7]{0,1,2:T(1,128)} %param.10) | copy-start | bytes 1348
  7.3 224.1 %copy-start.2 = (s32[4,1,4]{2,1,0:T(1,128)S(1)}, s32[4,1,4]{2,1,0:T(1,128)}, u32[]{:S(2)}) copy-start(s32[4,1,4]{2,1,0:T(1,128)} %param.11) | copy-start | bytes 196
  7.3 224.1 %all-gather.3.cloned.1.call-start = ((), (), s32[]{:S(2)}) async-start(), calls=%async_computation | async-start | bytes 36700160 | tf_op jit(solution)/shard_map/all_gather | solution.py:32
  8.0 339.4 %all-reduce.3.cloned.1.call-start = ((), (), s32[]{:S(2)}) async-start(), calls=%async_computation.2 | async-start | bytes 2097152
  231.4 75.8 %copy-start.3 = (u32[32]{0:T(128)S(1)}, u32[32]{0:T(128)}, u32[]{:S(2)}) copy-start(u32[32]{0:T(128)} %constant.166) | copy-start | bytes 388
Sparse Core Ops, SparseCore 0:
  8.9 44.0 all-gather.4
  54.6 176.7 all-gather.2
  307.3 40.0 all-reduce.2
where the time goes:
time: 356 us
  waiting for transfers between devices  246 us (69%)
  local copies, waits for them, and re-layouts  61.7 us (17%)
  blocking collectives  17.8 us (5%)
  between operations  13.8 us (4%)
  matrix products  11.1 us (3%)
  other arithmetic  5.41 us (2%)
    all_gather x1, waiting for transfers between devices, on_device(): lax.all_gather(b_tiles, 'row', axis=0, tiled=True)  178 us
    gather x8, local copies, waits for them, and re-layouts, row_block(): chosen = jnp.take(b_flat, flat_index.reshape(-1), axis=0)  52.3 us
    unnamed x4, waiting for transfers between devices  40.4 us
    all_gather x1, waiting for transfers between devices, on_device(): a_piece = lax.all_gather(a_tiles, 'col', axis=0, tiled=True)  27 us
    all_gather x1, blocking collectives, on_device(): index_piece = lax.all_gather(a_cols, 'col', axis=0, tiled=True)  12.6 us
    dot_general x4, matrix products, row_block(): jnp.einsum('heab,qhebc->qac', a_row, chosen, precision=lax.Precision.HIGH...  11.1 us
  transfers between devices with their start and end apart: 3, of which 3 were waited for; matrix products, arithmetic and copies ran while one was open for 0% of the time, Pallas kernels for 0%

commit v1 on v0

--- a/solution.py
+++ b/solution.py
@@ -33,7 +33,12 @@
         lax.all_gather(b_rows, "row", axis=0, tiled=True),
     )
     b_flat = b_panel.reshape((-1,) + b_panel.shape[3:])
-    a_piece = lax.all_gather(a_tiles, "col", axis=0, tiled=True)
+    ring = [a_tiles]
+    for hop in range(3):
+        ring.append(lax.ppermute(ring[-1], "col", [(dev, (dev + 1) % 4) for dev in range(4)]))
+    a_piece = jnp.roll(
+        jnp.concatenate(ring[::-1], axis=0), (lax.axis_index("col") + 1) * ring[0].shape[0], axis=0
+    )
     index_piece = lax.all_gather(a_cols, "col", axis=0, tiled=True)
 
     def one_row(inputs):

time: 356 us -> 315 us (0.88)
  waiting for transfers between devices: 246 us -> 197 us
    all_gather x1, waiting for transfers between devices: 178 us -> 131 us  [on_device(): lax.all_gather(b_tiles, 'row', axis=0, tiled=True)]
    all_gather x1 -> x0, waiting for transfers between devices: 27 us -> none  [on_device(): a_piece = lax.all_gather(a_tiles, 'col', axis=0, tiled=True)]
    ppermute x0 -> x3, waiting for transfers between devices: none -> 26 us  [on_device(): lax.ppermute(ring[-1], 'col', [(dev, (dev + 1) % 4) for dev in range(4)])]
    unnamed x4 -> x3, waiting for transfers between devices: 40.4 us -> 39.7 us
  transfers between devices with their start and end apart: 3 -> 5, of which waited for: 3 -> 4; matrix products, arithmetic and copies ran while one was open for 0% -> 1% of each run, Pallas kernels for 0% -> 0%
where the time goes in v1:
time: 315 us
  waiting for transfers between devices  197 us (63%)
  local copies, waits for them, and re-layouts  63.6 us (20%)
  blocking collectives  19.9 us (6%)
  between operations  14.1 us (4%)
  matrix products  11.3 us (4%)
  other arithmetic  5.38 us (2%)
    all_gather x1, waiting for transfers between devices, on_device(): lax.all_gather(b_tiles, 'row', axis=0, tiled=True)  131 us
    gather x8, local copies, waits for them, and re-layouts, row_block(): chosen = jnp.take(b_flat, flat_index.reshape(-1), axis=0)  52.3 us
    unnamed x3, waiting for transfers between devices  39.7 us
    ppermute x3, waiting for transfers between devices, on_device(): lax.ppermute(ring[-1], 'col', [(dev, (dev + 1) % 4) for dev in range(4)])  26 us
    all_gather x1, blocking collectives, on_device(): index_piece = lax.all_gather(a_cols, 'col', axis=0, tiled=True)  14.5 us
    dot_general x4, matrix products, row_block(): jnp.einsum('heab,qhebc->qac', a_row, chosen, precision=lax.Precision.HIGH...  11.3 us
  transfers between devices with their start and end apart: 5, of which 4 were waited for; matrix products, arithmetic and copies ran while one was open for 1% of the time, Pallas kernels for 0%

profile of v1, /device:TPU:0, one launch (start us, length us, event | category | flops | bytes accessed | tf_op | source)
XLA Modules:
  0.0 314.8 jit_solution(1192702088288874146)
XLA Ops:
  7.6 3.1 collective-permute-start
  10.6 12.5 %collective-permute-done = f32[1,1,7,128,128]{4,3,2,1,0:T(8,128)S(1)} collective-permute-done((f32[1,1,7,128,128]{4,3,2,1,0:T(8,128)S(1)}, f32[1,1,7,128,128]{4,3,2,1,0:T(8,128)S(1)}, u32[]{:S(2)}, u32[]{:S(2)}) %collective-permute-start) | collective-permute-done | bytes 458784 | tf_op jit(solution)/shard_map/ppermute | solution.py:38
  23.2 13.5 %collective-permute-done.1 = f32[1,1,7,128,128]{4,3,2,1,0:T(8,128)S(1)} collective-permute-done((f32[1,1,7,128,128]{4,3,2,1,0:T(8,128)S(1)}, f32[1,1,7,128,128]{4,3,2,1,0:T(8,128)S(1)}, u32[]{:S(2)}, u32[]{:S(2)}) %collective-permute-start.1) | collective-permute-done | bytes 458784 | tf_op jit(solution)/shard_map/ppermute | solution.py:38
  36.6 14.5 %all_gather.10 = s32[4,1,7]{2,1,0:T(1,128)S(1)} all-gather(s32[1,1,7]{2,1,0:T(1,128)S(1)} %copy-done.2), channel_id=1, replica_groups=mesh['row'=4,'col'=4,'layer'=2] {'col'}, dimensions={0}, use_global_device_ids=true | all-gather | bytes 140 | tf_op jit(solution)/shard_map/all_gather | solution.py:42
  51.2 5.5 %all_gather.9 = s32[64,1,7]{2,0,1:T(8,128)S(1)} all-gather(s32[16,1,7]{2,0,1:T(8,128)S(1)} %copy.18), channel_id=1, replica_groups=mesh['row'=4,'col'=4,'layer'=2] {'row'}, dimensions={0}, use_global_device_ids=true | all-gather | bytes 2240 | tf_op jit(solution)/shard_map/all_gather | solution.py:33
  57.0 1.5 constant_dynamic-slice_fusion.3
  58.5 131.4 %all-gather.2.cloned.1.call-done = f32[64,1,7,128,128]{4,3,2,1,0:T(8,128)} async-done(((f32[16,1,7,128,128]{4,3,2,1,0:T(8,128)}), f32[64,1,7,128,128]{4,3,2,1,0:T(8,128)}) %all-gather.2.cloned.1.call-update) | async-done | bytes 29360144 | tf_op jit(solution)/shard_map/all_gather | solution.py:32
  189.8 76.0 %while.13 = (s32[]{:T(128)}, f32[4,4,128,128]{3,2,1,0:T(8,128)}, s32[4,4]{1,0:T(4,128)S(1)}, s32[64,1,7]{2,0,1:T(8,128)S(1)}, s32[4,1,7]{2,1,0:T(1,128)S(1)}, /*...) while((s32[]{:T(128)}, f32[4,4,128,128]{3,2,1,0:T(8,128)}, s32[4,4]{1,0:T(4,128)S(1)}, ...), condition=%wide.region_3.4_spmd, body=%wide.region_0.3_spmd.sunk | while | flops 705565312 | bytes 10956058 | solution.py:47
  190.4 1.0 iota_reduce_fusion.2
  191.6 11.3 %gather_fusion.1 = f32[28,128,128]{2,1,0:T(8,128)} fusion(f32[448,128,128]{2,1,0:T(8,128)} %get-tuple-element.214, s32[1024]{0:T(1024)S(1)} %pad_clamp_fusion.5), kind=kCustom, calls=%fused_computation.1.clone.1 | custom fusion | bytes 3670128 | tf_op jit(solution)/shard_map/while/body/eval_jaxpr/jit(_take)/gather | solution.py:21
  202.9 1.8 copy.30
  205.1 2.8 fusion.36
  209.4 1.0 iota_reduce_fusion.2
  210.6 11.3 %gather_fusion.1 = f32[28,128,128]{2,1,0:T(8,128)} fusion(f32[448,128,128]{2,1,0:T(8,128)} %get-tuple-element.214, s32[1024]{0:T(1024)S(1)} %pad_clamp_fusion.5), kind=kCustom, calls=%fused_computation.1.clone.1 | custom fusion | bytes 3670128 | tf_op jit(solution)/shard_map/while/body/eval_jaxpr/jit(_take)/gather | solution.py:21
  221.9 1.8 copy.30
  224.1 2.8 fusion.36
  229.6 11.3 %gather_fusion.1 = f32[28,128,128]{2,1,0:T(8,128)} fusion(f32[448,128,128]{2,1,0:T(8,128)} %get-tuple-element.214, s32[1024]{0:T(1024)S(1)} %pad_clamp_fusion.5), kind=kCustom, calls=%fused_computation.1.clone.1 | custom fusion | bytes 3670128 | tf_op jit(solution)/shard_map/while/body/eval_jaxpr/jit(_take)/gather | solution.py:21
  240.9 1.8 copy.30
  243.1 2.8 fusion.36
  248.6 11.3 %gather_fusion.1 = f32[28,128,128]{2,1,0:T(8,128)} fusion(f32[448,128,128]{2,1,0:T(8,128)} %get-tuple-element.214, s32[1024]{0:T(1024)S(1)} %pad_clamp_fusion.5), kind=kCustom, calls=%fused_computation.1.clone.1 | custom fusion | bytes 3670128 | tf_op jit(solution)/shard_map/while/body/eval_jaxpr/jit(_take)/gather | solution.py:21
  259.9 1.8 copy.30
  262.1 2.8 fusion.36
  267.1 39.0 %all-reduce.3.cloned.1.call-done = f32[4,1,4,128,128]{4,3,2,1,0:T(8,128)} async-done(((f32[4,1,4,128,128]{4,3,2,1,0:T(8,128)}), f32[4,1,4,128,128]{4,3,2,1,0:T(8,128)}) %all-reduce.3.cloned.1.call-update) | async-done | bytes 1048592
  306.1 1.9 constant_dynamic-slice_fusion.2
  (90 shorter events, 12.2 us)
Async XLA Ops:
  6.5 1.0 copy-start
  6.5 30.1 %copy-start.2 = (s32[1,1,7]{2,1,0:T(1,128)S(1)}, s32[1,1,7]{2,1,0:T(1,128)}, u32[]{:S(2)}) copy-start(s32[1,1,7]{2,1,0:T(1,128)} %param.8) | copy-start | bytes 88
  6.5 44.6 %copy-start.1 = (s32[16,1,7]{0,1,2:T(1,128)S(1)}, s32[16,1,7]{0,1,2:T(1,128)}, u32[]{:S(2)}) copy-start(s32[16,1,7]{0,1,2:T(1,128)} %param.10) | copy-start | bytes 1348
  6.5 183.3 %all-gather.2.cloned.1.call-start = ((), (), s32[]{:S(2)}) async-start(), calls=%async_computation | async-start | bytes 36700160 | tf_op jit(solution)/shard_map/all_gather | solution.py:32
  7.3 298.8 %all-reduce.3.cloned.1.call-start = ((), (), s32[]{:S(2)}) async-start(), calls=%async_computation.1 | async-start | bytes 2097152
  7.6 15.6 %collective-permute-start = (f32[1,1,7,128,128]{4,3,2,1,0:T(8,128)S(1)}, f32[1,1,7,128,128]{4,3,2,1,0:T(8,128)S(1)}, u32[]{:S(2)}, u32[]{:S(2)}) collective-permute-start(f32[1,1,7,128,128]{4,3,2,1,0:T(8,128)S(1)} %copy-done), channel_id=1, source_target_pairs={{0,2},{2,4},{4,6},{6,0},{1,3},{3,5},{5,7},{7,1},{8,10},{10,12},{12... | collective-permute-start | bytes 1376264 | tf_op jit(solution)/shard_map/ppermute | solution.py:38
  23.1 13.5 %collective-permute-start.1 = (f32[1,1,7,128,128]{4,3,2,1,0:T(8,128)S(1)}, f32[1,1,7,128,128]{4,3,2,1,0:T(8,128)S(1)}, u32[]{:S(2)}, u32[]{:S(2)}) collective-permute-start(f32[1,1,7,128,128]{4,3,2,1,0:T(8,128)S(1)} %collective-permute-done), channel_id=1, source_target_pairs={{0,2},{2,4},{4,6},{6,0},{1,3},{3,5},{5,7},{7,1},{8,10},{10,12},{12... | collective-permute-start | bytes 1376264 | tf_op jit(solution)/shard_map/ppermute | solution.py:38
  36.6 20.0 %collective-permute-start.2 = (f32[1,1,7,128,128]{4,3,2,1,0:T(8,128)S(1)}, f32[1,1,7,128,128]{4,3,2,1,0:T(8,128)S(1)}, u32[]{:S(2)}, u32[]{:S(2)}) collective-permute-start(f32[1,1,7,128,128]{4,3,2,1,0:T(8,128)S(1)} %collective-permute-done.1), channel_id=1, source_target_pairs={{0,2},{2,4},{4,6},{6,0},{1,3},{3,5},{5,7},{7,1},{8,10},{10,12},{12... | collective-permute-start | bytes 1376264 | tf_op jit(solution)/shard_map/ppermute | solution.py:38
  56.8 133.0 %copy-start.3 = (s32[4,1,4]{2,1,0:T(1,128)S(1)}, s32[4,1,4]{2,1,0:T(1,128)}, u32[]{:S(2)}) copy-start(s32[4,1,4]{2,1,0:T(1,128)} %param.11) | copy-start | bytes 196
  189.8 76.0 %copy-start.4 = (u32[32]{0:T(128)S(1)}, u32[32]{0:T(128)}, u32[]{:S(2)}) copy-start(u32[32]{0:T(128)} %constant.195) | copy-start | bytes 388
Sparse Core Ops, SparseCore 0:
  8.9 180.8 all-gather.1
  266.0 40.0 all-reduce.2
